TPU v7x, 256 devices: a 2x2x32 block of a 4x8x32 slice. The times are simulated.
256 devices in a mesh: rep: 4 (over y, x), section: 2 (over core), wide: 32 (over z).
Axes of the slice: x: 2, y: 2, z: 32, core: 2. Of those that a mesh axis runs over, the one named last changes fastest.
The devices are a block of a 4x8x32 slice.
Arguments:
- acts: bfloat16 [2, 1024, 8192], P('section', 'rep', 'wide'), parts along dimension 1, may hold values from -100 to 100
- norm_gain: bfloat16 [2, 8192], P('section', 'wide'), may hold values from 0.099609375 to 1.8984375
- w_qkv: bfloat16 [2, 8192, 5120], P('section', None, 'wide'), may hold values from -0.0625 to 0.0625
- w_out: bfloat16 [2, 4096, 8192], P('section', None, 'wide'), may hold values from -0.5 to 0.5
- key_cache: bfloat16 [2, 1024, 384, 512], P('section', ('rep', 'wide')), parts along dimension 1, may hold values from -400 to 400
- value_cache: bfloat16 [2, 1024, 384, 512], P('section', ('rep', 'wide')), parts along dimension 1, may hold values from -6 to 6
- cache_lengths: int32 [2, 1024], P('section', ('rep', 'wide')), parts along dimension 1, may hold values from 2 to 384, as said below
- slot_of: int32 [2, 1024], P('section', 'rep'), parts along dimension 1, may hold values from 0 to 255, each once within a row
Outputs:
- handed: bfloat16 [2, 1024, 8192], P('section', 'rep', 'wide'), parts along dimension 1
There are 4 independent parts, one for each index of `rep`. A program takes and returns all parts, laid end to end along the dimension named above; an argument that names none is the same for every part. Nothing has to cross between parts.
Inputs may be any that keep to these rules, and one draw needn't show every extreme that they name: `cache_lengths`: slot j of a section belongs to owner j // 8; in every section some slot holds exactly 384. `slot_of`: each section's row names every slot once.
All inputs are finite; a program needn't handle non-finite values.
Results may differ from a plain program's by a relative error of at most 0.005.
Values may be sent and summed in bfloat16 or wider, within the bound.
No kernel may reach another device: no remote copies, remote signals or barrier semaphores. Data moves between devices by JAX's collectives and lax.ppermute only.
A program may use at most 64 MiB of HBM per device.

v0:
```python
import math
import jax
import jax.numpy as jnp
from jax import lax
from jax.sharding import PartitionSpec as P

D = 8192
HEADS = 32
KV_HEADS = 4
HDIM = 128
epsilon = 1e-05
rope_base = 500000.0
masked_score = -1e30


def copy_for_each(value, axis):
    count = lax.axis_size(axis)
    return lax.all_to_all(
        jnp.broadcast_to(value[None], (count, *value.shape)), axis, 0, 0, tiled=True
    )


def of_everyone(value, axis):
    return copy_for_each(value, axis).sum(axis=0)


def passed_along(value, axis, steps):
    count = lax.axis_size(axis)
    pairs = [(source, (source + steps) % count) for source in range(count)]
    return lax.ppermute(value, axis, pairs)


def rotate(values, position):
    half_dim = HDIM // 2
    exponent = jnp.arange(half_dim, dtype=jnp.float32) * (2.0 / HDIM)
    frequency = jnp.exp(-math.log(rope_base) * exponent)
    angle = position[..., None] * frequency
    cosine = jnp.cos(angle)
    sine = jnp.sin(angle)
    first_half = values[..., :half_dim]
    second_half = values[..., half_dim:]
    return jnp.concatenate(
        [first_half * cosine - second_half * sine, second_half * cosine + first_half * sine],
        axis=-1,
    )


def attend(joined_rows, key_rows, value_rows, lengths_here):
    row_count = joined_rows.shape[0]
    groups = HEADS // KV_HEADS
    query_width = HEADS * HDIM
    kv_width = KV_HEADS * HDIM
    queries = joined_rows[:, :query_width].reshape(row_count, KV_HEADS, groups, HDIM)
    new_keys = joined_rows[:, query_width : query_width + kv_width].reshape(
        row_count, KV_HEADS, HDIM
    )
    new_values = joined_rows[:, query_width + kv_width :].reshape(row_count, KV_HEADS, HDIM)
    position = lengths_here.astype(jnp.float32)
    queries = rotate(queries.astype(jnp.float32), position[:, None, None]).astype(jnp.bfloat16)
    new_keys = rotate(new_keys.astype(jnp.float32), position[:, None]).astype(jnp.bfloat16)
    score_scale = 1.0 / math.sqrt(HDIM)
    cache_span = key_rows.shape[1]
    cached_keys = key_rows.reshape(row_count, cache_span, KV_HEADS, HDIM)
    cached_values = value_rows.reshape(row_count, cache_span, KV_HEADS, HDIM)
    own_score = (
        jnp.einsum("ngqd,ngd->ngq", queries, new_keys, preferred_element_type=jnp.float32)
        * score_scale
    )
    scores = (
        jnp.einsum("ngqd,nlgd->ngql", queries, cached_keys, preferred_element_type=jnp.float32)
        * score_scale
    )
    live_mask = (jnp.arange(cache_span, dtype=jnp.int32)[None, :] < lengths_here[:, None])[
        :, None, None, :
    ]
    masked = jnp.where(live_mask, scores, masked_score)
    peak = jnp.maximum(jnp.max(masked, axis=-1), own_score)
    weights = jnp.where(live_mask, jnp.exp(masked - peak[..., None]), 0.0)
    sums = jnp.sum(weights, axis=-1)
    weighted = jnp.einsum(
        "ngql,nlgd->ngqd",
        weights.astype(jnp.bfloat16),
        cached_values,
        preferred_element_type=jnp.float32,
    )
    own_weight = jnp.exp(own_score - peak)
    denominator = sums + own_weight
    own_rounded = own_weight.astype(jnp.bfloat16).astype(jnp.float32)
    weighted = weighted + own_rounded[..., None] * new_values.astype(jnp.float32)[:, :, None, :]
    return (weighted / denominator[..., None]).reshape(row_count, query_width).astype(jnp.bfloat16)


def shards(acts, norm_gain, w_qkv, w_out, key_cache, value_cache, cache_lengths, slot_of):
    tokens = acts[0].astype(jnp.float32)
    squares = of_everyone(jnp.sum(tokens * tokens, axis=1), "wide")
    normed = (
        tokens * lax.rsqrt(squares / D + epsilon)[:, None] * norm_gain[0].astype(jnp.float32)
    ).astype(jnp.bfloat16)
    slot_table = slot_of[0]
    request_total = slot_table.shape[0]
    request_at_slot = (
        jnp.zeros((request_total,), jnp.int32)
        .at[slot_table]
        .set(jnp.arange(request_total, dtype=jnp.int32))
    )
    projection = w_qkv[0]
    whole = lax.all_gather(normed, "wide", axis=1, tiled=True)
    columns = jnp.dot(whole, projection, preferred_element_type=jnp.float32).astype(jnp.bfloat16)
    joined_rows = lax.all_to_all(
        columns[request_at_slot], "wide", split_axis=0, concat_axis=1, tiled=True
    )
    attended = attend(joined_rows, key_cache[0], value_cache[0], cache_lengths[0])
    out_weight = w_out[0]
    projected = jnp.dot(
        lax.all_gather(attended, "wide", axis=0, tiled=True),
        out_weight,
        preferred_element_type=jnp.float32,
    )
    updated = (tokens + projected[slot_table]).astype(jnp.bfloat16)
    return passed_along(updated[None], "section", 1)


def solution(mesh):
    placed = (
        P("section", "rep", "wide"),
        P("section", "wide"),
        P("section", None, "wide"),
        P("section", None, "wide"),
        P("section", ("rep", "wide"), None, None),
        P("section", ("rep", "wide"), None, None),
        P("section", ("rep", "wide")),
        P("section", "rep"),
    )
    return jax.shard_map(
        shards, mesh=mesh, in_specs=placed, out_specs=P("section", "rep", "wide"), check_vma=False
    )
```

profile of v0, /device:TPU:37, one launch (start us, length us, event | category | flops | bytes accessed | tf_op | source)
XLA Modules:
  0.0 379.6 jit_solution(14781178704558300775)
XLA Ops:
  6.5 0.0 copy-start
  6.6 1.2 fusion.33
  7.7 0.6 broadcast_in_dim.23
  8.4 33.2 %all-to-all-start = ((f32[32,1,256]{2,1,0:T(1,128)}), f32[32,1,256]{2,1,0:T(1,128)S(1)}, u32[]{:S(2)}, u32[]{:S(2)}) async-start(f32[32,1,256]{2,1,0:T(1,128)} %broadcast_in_dim.23), calls=%async_computation | async-start | bytes 65536 | tf_op jit(solution)/shard_map/all_to_all | solution.py:18
  41.6 0.1 all-gather.3.cloned.1.call-start
  41.6 0.7 mul.188
  42.3 20.6 %all-to-all-done = f32[32,1,256]{2,1,0:T(1,128)S(1)} async-done(((f32[32,1,256]{2,1,0:T(1,128)}), f32[32,1,256]{2,1,0:T(1,128)S(1)}, u32[]{:S(2)}, u32[]{:S(2)}) %all-to-all-start) | async-done | bytes 32800 | tf_op jit(solution)/shard_map/all_to_all | solution.py:18
  63.0 0.1 reduce_sum.28
  63.0 1.7 fusion.35
  64.7 0.1 all-gather.3.cloned.1.call-update
  64.8 5.5 %reshape_squeeze.6 = bf16[8,384,4,128]{3,2,1,0:T(4,128)(2,1)} reshape(bf16[1,8,384,512]{3,2,1,0:T(8,128)(2,1)} %param.12) | data formatting | bytes 6291456 | tf_op jit(solution)/shard_map/reshape;squeeze | solution.py:63
  70.3 0.0 copy-start.3
  70.3 5.5 %reshape_squeeze.7 = bf16[8,384,4,128]{3,2,1,0:T(4,128)(2,1)} reshape(bf16[1,8,384,512]{3,2,1,0:T(8,128)(2,1)} %param.13) | data formatting | bytes 6291456 | tf_op jit(solution)/shard_map/reshape;squeeze | solution.py:64
  75.8 0.0 copy-done.3
  75.8 1.4 scatter_custom_fusion
  77.3 0.0 copy-start.4
  77.3 100.0 %all-gather.3.cloned.1.call-done = bf16[256,8192]{1,0:T(8,128)(2,1)} async-done(((bf16[256,256]{1,0:T(8,128)(2,1)}), bf16[256,8192]{1,0:T(8,128)(2,1)}) %all-gather.3.cloned.1.call-update) | async-done | bytes 4194320 | tf_op jit(solution)/shard_map/all_gather | solution.py:107
  177.3 0.0 copy-done
  177.3 3.7 fusion.20
  181.0 0.1 copy.25
  181.1 1.8 gather_fusion
  183.0 12.1 %all-to-all-start.1 = ((bf16[32,8,160]{2,1,0:T(8,128)(2,1)}), bf16[32,8,160]{2,1,0:T(8,128)(2,1)S(1)}, u32[]{:S(2)}, u32[]{:S(2)}) async-start(bf16[32,8,160]{2,1,0:T(8,128)(2,1)} %bitcast.6), calls=%async_computation.1 | async-start | bytes 262144 | tf_op jit(solution)/shard_map/all_to_all | solution.py:109
  195.1 0.1 all-gather.5.cloned.1.call-start
  195.1 0.0 copy-done.4
  195.2 0.1 iota_compare_fusion
  195.2 0.1 multiply_cosine_fusion
  195.3 25.2 %all-to-all-done.1 = bf16[32,8,160]{2,1,0:T(8,128)(2,1)S(1)} async-done(((bf16[32,8,160]{2,1,0:T(8,128)(2,1)}), bf16[32,8,160]{2,1,0:T(8,128)(2,1)S(1)}, u32[]{:S(2)}, u32[]{:S(2)}) %all-to-all-start.1) | async-done | bytes 81952 | tf_op jit(solution)/shard_map/all_to_all | solution.py:109
  220.5 0.2 all_to_all.22
  220.7 0.0 copy-start.1
  220.8 0.1 subtract_convert_fusion.1
  220.9 0.1 subtract_convert_fusion
  221.0 0.1 maximum_bitcast_fusion
  221.1 0.2 fusion.41
  221.3 3.5 fusion.51
  224.8 0.2 fusion.31
  225.1 0.0 copy-done.1
  225.1 0.7 fusion.26
  225.9 0.7 copy.58
  226.5 0.1 all-gather.5.cloned.1.call-update
  226.6 0.0 copy-start.2
  226.6 118.5 %all-gather.5.cloned.1.call-done = bf16[256,4096]{1,0:T(8,128)(2,1)} async-done(((bf16[8,4096]{1,0:T(8,128)(2,1)}), bf16[256,4096]{1,0:T(8,128)(2,1)}) %all-gather.5.cloned.1.call-update) | async-done | bytes 2097168 | tf_op jit(solution)/shard_map/all_gather | solution.py:115
  345.1 2.9 fusion.6
  348.0 1.0 gather_fusion.1
  349.0 0.0 copy-done.2
  349.0 22.1 %collective-permute-start = (bf16[1,256,256]{2,1,0:T(8,128)(2,1)S(1)}, bf16[1,256,256]{2,1,0:T(8,128)(2,1)S(1)}, u32[]{:S(2)}, u32[]{:S(2)}) collective-permute-start(bf16[1,256,256]{2,1,0:T(8,128)(2,1)S(1)} %fusion.36), channel_id=1, source_target_pairs={{0,32},{32,0},{1,33},{33,1},{2,34},{34,2},{3,35},{35,3},{4,36},{36... | collective-permute-start | bytes 393224 | tf_op jit(solution)/shard_map/ppermute | solution.py:30
  371.1 1.0 collective-permute-done
  372.1 0.7 copy.60
  (16 shorter events, 0.2 us)
Async XLA Ops:
  6.5 170.8 %copy-start = (bf16[1,8192,160]{1,2,0:T(8,128)(2,1)S(1)}, bf16[1,8192,160]{1,2,0:T(8,128)(2,1)}, u32[]{:S(2)}) copy-start(bf16[1,8192,160]{1,2,0:T(8,128)(2,1)} %param.10) | copy-start | bytes 7864324
  8.4 54.6 %all-to-all-start = ((f32[32,1,256]{2,1,0:T(1,128)}), f32[32,1,256]{2,1,0:T(1,128)S(1)}, u32[]{:S(2)}, u32[]{:S(2)}) async-start(f32[32,1,256]{2,1,0:T(1,128)} %broadcast_in_dim.23), calls=%async_computation | async-start | bytes 65536 | tf_op jit(solution)/shard_map/all_to_all | solution.py:18
  41.6 135.7 %all-gather.3.cloned.1.call-start = ((), (), s32[]{:S(2)}) async-start(), calls=%async_computation.2 | async-start | bytes 4325376 | tf_op jit(solution)/shard_map/all_gather | solution.py:107
  70.3 5.6 %copy-start.3 = (s32[1,256]{1,0:T(1,128)S(1)}, s32[1,256]{1,0:T(1,128)}, u32[]{:S(2)}) copy-start(s32[1,256]{1,0:T(1,128)} %param.15) | copy-start | bytes 3076
  77.3 117.9 %copy-start.4 = (s32[1,8]{1,0:T(1,128)S(1)}, s32[1,8]{1,0:T(1,128)}, u32[]{:S(2)}) copy-start(s32[1,8]{1,0:T(1,128)} %param.14) | copy-start | bytes 100
  183.0 37.6 %all-to-all-start.1 = ((bf16[32,8,160]{2,1,0:T(8,128)(2,1)}), bf16[32,8,160]{2,1,0:T(8,128)(2,1)S(1)}, u32[]{:S(2)}, u32[]{:S(2)}) async-start(bf16[32,8,160]{2,1,0:T(8,128)(2,1)} %bitcast.6), calls=%async_computation.1 | async-start | bytes 262144 | tf_op jit(solution)/shard_map/all_to_all | solution.py:109
  195.1 150.0 %all-gather.5.cloned.1.call-start = ((), (), s32[]{:S(2)}) async-start(), calls=%async_computation.3 | async-start | bytes 2162688 | tf_op jit(solution)/shard_map/all_gather | solution.py:115
  220.7 4.4 %copy-start.1 = (bf16[8,384,4,128]{3,2,1,0:T(4,128)(2,1)S(1)}, bf16[8,384,4,128]{3,2,1,0:T(4,128)(2,1)}, u32[]{:S(2)}) copy-start(bf16[8,384,4,128]{3,2,1,0:T(4,128)(2,1)} %reshape_squeeze.7) | copy-start | bytes 9437188
  226.6 122.4 %copy-start.2 = (bf16[1,256,256]{2,1,0:T(8,128)(2,1)S(1)}, bf16[1,256,256]{2,1,0:T(8,128)(2,1)}, u32[]{:S(2)}) copy-start(bf16[1,256,256]{2,1,0:T(8,128)(2,1)} %param.8) | copy-start | bytes 393220
  349.0 23.1 %collective-permute-start = (bf16[1,256,256]{2,1,0:T(8,128)(2,1)S(1)}, bf16[1,256,256]{2,1,0:T(8,128)(2,1)S(1)}, u32[]{:S(2)}, u32[]{:S(2)}) collective-permute-start(bf16[1,256,256]{2,1,0:T(8,128)(2,1)S(1)} %fusion.36), channel_id=1, source_target_pairs={{0,32},{32,0},{1,33},{33,1},{2,34},{34,2},{3,35},{35,3},{4,36},{36... | collective-permute-start | bytes 393224 | tf_op jit(solution)/shard_map/ppermute | solution.py:30
Sparse Core Ops, SparseCore 0:
  64.9 112.3 all-gather.2
  226.7 118.3 all-gather.4
where the time goes:
time: 380 us
  waiting for transfers between devices  265 us (70%)
  starting transfers between devices  67.5 us (18%)
  local copies, waits for them, and re-layouts  17.6 us (5%)
  between operations  13.7 us (4%)
  matrix products  11.1 us (3%)
  other arithmetic  4.37 us (1%)
    all_gather x1, waiting for transfers between devices, shards(): lax.all_gather(attended, 'wide', axis=0, tiled=True)  118 us
    all_gather x1, waiting for transfers between devices, shards(): whole = lax.all_gather(normed, 'wide', axis=1, tiled=True)  100 us
    all_to_all x1, starting transfers between devices, copy_for_each(): lax.all_to_all(jnp.broadcast_to(value[None], (count, *value.shape)), axis...  33.2 us
    all_to_all x1, waiting for transfers between devices, shards(): lax.all_to_all(columns[request_at_slot], 'wide', split_axis=0, concat_axi...  25.2 us
    ppermute x1, starting transfers between devices, passed_along(): return lax.ppermute(value, axis, pairs)  22.1 us
    all_to_all x1, waiting for transfers between devices, copy_for_each(): lax.all_to_all(jnp.broadcast_to(value[None], (count, *value.shape)), axis...  20.6 us
    all_to_all x1, starting transfers between devices, shards(): lax.all_to_all(columns[request_at_slot], 'wide', split_axis=0, concat_axi...  12.1 us
  transfers between devices with their start and end apart: 5, of which 5 were waited for; matrix products, arithmetic and copies ran while one was open for 4% of the time, Pallas kernels for 0%

commit v1 on v0

--- a/solution.py
+++ b/solution.py
@@ -11,6 +11,13 @@
 epsilon = 1e-05
 rope_base = 500000.0
 masked_score = -1e30
+
+
+def exchange_gather(x, name, dim):
+    size = lax.axis_size(name)
+    tiles = jnp.stack([x for _ in range(size)])
+    tiles = lax.all_to_all(tiles, name, split_axis=0, concat_axis=0)
+    return jnp.concatenate(tiles, axis=dim)
 
 
 def copy_for_each(value, axis):
@@ -112,9 +119,7 @@
     attended = attend(joined_rows, key_cache[0], value_cache[0], cache_lengths[0])
     out_weight = w_out[0]
     projected = jnp.dot(
-        lax.all_gather(attended, "wide", axis=0, tiled=True),
-        out_weight,
-        preferred_element_type=jnp.float32,
+        exchange_gather(attended, "wide", 0), out_weight, preferred_element_type=jnp.float32
     )
     updated = (tokens + projected[slot_table]).astype(jnp.bfloat16)
     return passed_along(updated[None], "section", 1)

time: 380 us -> 447 us (1.18)
  waiting for transfers between devices: 265 us -> 328 us
    all_to_all x0 -> x1, waiting for transfers between devices: none -> 181 us  [exchange_gather(): tiles = lax.all_to_all(tiles, name, split_axis=0, concat_axis=0)]
    all_gather x1 -> x0, waiting for transfers between devices: 118 us -> none  [shards(): lax.all_gather(attended, 'wide', axis=0, tiled=True)]
    all_to_all x0 -> x1, starting transfers between devices: none -> 5.56 us  [exchange_gather(): tiles = lax.all_to_all(tiles, name, split_axis=0, concat_axis=0)]
  transfers between devices with their start and end apart: 5 -> 5, of which waited for: 5 -> 5; matrix products, arithmetic and copies ran while one was open for 4% -> 3% of each run, Pallas kernels for 0% -> 0%
where the time goes in v1:
time: 447 us; the launch traced here: 446 us
  waiting for transfers between devices  328 us (73%)
  starting transfers between devices  70 us (16%)
  local copies, waits for them, and re-layouts  18.5 us (4%)
  between operations  13.7 us (3%)
  matrix products  11.1 us (2%)
    all_to_all x1, waiting for transfers between devices, exchange_gather(): tiles = lax.all_to_all(tiles, name, split_axis=0, concat_axis=0)  181 us
    all_gather x1, waiting for transfers between devices, shards(): whole = lax.all_gather(normed, 'wide', axis=1, tiled=True)  100 us
    all_to_all x1, starting transfers between devices, copy_for_each(): lax.all_to_all(jnp.broadcast_to(value[None], (count, *value.shape)), axis...  33.2 us
    all_to_all x1, waiting for transfers between devices, shards(): lax.all_to_all(columns[request_at_slot], 'wide', split_axis=0, concat_axi...  25.2 us
    all_to_all x1, waiting for transfers between devices, copy_for_each(): lax.all_to_all(jnp.broadcast_to(value[None], (count, *value.shape)), axis...  20.6 us
    ppermute x1, starting transfers between devices, passed_along(): return lax.ppermute(value, axis, pairs)  19.1 us
    all_to_all x1, starting transfers between devices, shards(): lax.all_to_all(columns[request_at_slot], 'wide', split_axis=0, concat_axi...  12.1 us
  transfers between devices with their start and end apart: 5, of which 5 were waited for; matrix products, arithmetic and copies ran while one was open for 3% of the time, Pallas kernels for 0%

profile of v1, /device:TPU:37, one launch (start us, length us, event | category | flops | bytes accessed | tf_op | source)
XLA Modules:
  0.0 445.9 jit_solution(12549103719042522118)
XLA Ops:
  6.5 0.0 copy-start
  6.6 1.2 fusion.34
  7.7 0.6 broadcast_in_dim.23
  8.4 33.2 %all-to-all-start = ((f32[32,1,256]{2,1,0:T(1,128)}), f32[32,1,256]{2,1,0:T(1,128)S(1)}, u32[]{:S(2)}, u32[]{:S(2)}) async-start(f32[32,1,256]{2,1,0:T(1,128)} %broadcast_in_dim.23), calls=%async_computation | async-start | bytes 65536 | tf_op jit(solution)/shard_map/all_to_all | solution.py:25
  41.6 0.1 all-gather.2.cloned.1.call-start
  41.6 0.7 mul.188
  42.3 20.6 %all-to-all-done = f32[32,1,256]{2,1,0:T(1,128)S(1)} async-done(((f32[32,1,256]{2,1,0:T(1,128)}), f32[32,1,256]{2,1,0:T(1,128)S(1)}, u32[]{:S(2)}, u32[]{:S(2)}) %all-to-all-start) | async-done | bytes 32800 | tf_op jit(solution)/shard_map/all_to_all | solution.py:25
  63.0 0.1 reduce_sum.28
  63.0 1.7 fusion.36
  64.7 0.1 all-gather.2.cloned.1.call-update
  64.8 5.5 %reshape_squeeze.6 = bf16[8,384,4,128]{3,2,1,0:T(4,128)(2,1)} reshape(bf16[1,8,384,512]{3,2,1,0:T(8,128)(2,1)} %param.12) | data formatting | bytes 6291456 | tf_op jit(solution)/shard_map/reshape;squeeze | solution.py:70
  70.3 0.0 copy-start.3
  70.3 5.5 %reshape_squeeze.7 = bf16[8,384,4,128]{3,2,1,0:T(4,128)(2,1)} reshape(bf16[1,8,384,512]{3,2,1,0:T(8,128)(2,1)} %param.13) | data formatting | bytes 6291456 | tf_op jit(solution)/shard_map/reshape;squeeze | solution.py:71
  75.8 0.0 copy-done.3
  75.8 1.4 scatter_custom_fusion
  77.3 0.0 copy-start.4
  77.3 100.0 %all-gather.2.cloned.1.call-done = bf16[256,8192]{1,0:T(8,128)(2,1)} async-done(((bf16[256,256]{1,0:T(8,128)(2,1)}), bf16[256,8192]{1,0:T(8,128)(2,1)}) %all-gather.2.cloned.1.call-update) | async-done | bytes 4194320 | tf_op jit(solution)/shard_map/all_gather | solution.py:114
  177.3 0.0 copy-done
  177.3 3.7 fusion.21
  181.0 0.1 copy.25
  181.1 1.8 gather_fusion
  183.0 12.1 %all-to-all-start.1 = ((bf16[32,8,160]{2,1,0:T(8,128)(2,1)}), bf16[32,8,160]{2,1,0:T(8,128)(2,1)S(1)}, u32[]{:S(2)}, u32[]{:S(2)}) async-start(bf16[32,8,160]{2,1,0:T(8,128)(2,1)} %bitcast.6), calls=%async_computation.1 | async-start | bytes 262144 | tf_op jit(solution)/shard_map/all_to_all | solution.py:116
  195.1 0.0 copy-done.4
  195.1 0.1 iota_compare_fusion
  195.2 0.1 multiply_cosine_fusion
  195.3 25.2 %all-to-all-done.1 = bf16[32,8,160]{2,1,0:T(8,128)(2,1)S(1)} async-done(((bf16[32,8,160]{2,1,0:T(8,128)(2,1)}), bf16[32,8,160]{2,1,0:T(8,128)(2,1)S(1)}, u32[]{:S(2)}, u32[]{:S(2)}) %all-to-all-start.1) | async-done | bytes 81952 | tf_op jit(solution)/shard_map/all_to_all | solution.py:116
  220.5 0.2 all_to_all.25
  220.7 0.0 copy-start.1
  220.8 0.1 subtract_convert_fusion.1
  220.9 0.1 subtract_convert_fusion
  221.0 0.1 maximum_bitcast_fusion
  221.1 0.2 fusion.42
  221.3 3.5 fusion.52
  224.8 0.2 fusion.32
  225.1 0.0 copy-done.1
  225.1 0.7 fusion.27
  225.9 1.5 stack.2
  227.5 5.6 %all-to-all-start.2 = ((bf16[32,8,4096]{2,1,0:T(8,128)(2,1)}), bf16[32,8,4096]{2,1,0:T(8,128)(2,1)}, u32[]{:S(2)}, u32[]{:S(2)}) async-start(bf16[32,8,4096]{2,1,0:T(8,128)(2,1)} %stack.2), calls=%async_computation.2 | async-start | bytes 4194304 | tf_op jit(solution)/shard_map/all_to_all | solution.py:19
  233.0 0.0 copy-start.2
  233.1 181.4 %all-to-all-done.2 = bf16[32,8,4096]{2,1,0:T(8,128)(2,1)} async-done(((bf16[32,8,4096]{2,1,0:T(8,128)(2,1)}), bf16[32,8,4096]{2,1,0:T(8,128)(2,1)}, u32[]{:S(2)}, u32[]{:S(2)}) %all-to-all-start.2) | async-done | bytes 2097184 | tf_op jit(solution)/shard_map/all_to_all | solution.py:19
  414.4 2.9 fusion.6
  417.3 1.0 gather_fusion.1
  418.3 0.0 copy-done.2
  418.4 19.1 %collective-permute-start = (bf16[1,256,256]{2,1,0:T(8,128)(2,1)S(1)}, bf16[1,256,256]{2,1,0:T(8,128)(2,1)S(1)}, u32[]{:S(2)}, u32[]{:S(2)}) collective-permute-start(bf16[1,256,256]{2,1,0:T(8,128)(2,1)S(1)} %fusion.37), channel_id=1, source_target_pairs={{0,32},{32,0},{1,33},{33,1},{2,34},{34,2},{3,35},{35,3},{4,36},{36... | collective-permute-start | bytes 393224 | tf_op jit(solution)/shard_map/ppermute | solution.py:37
  437.4 1.0 collective-permute-done
  438.4 0.7 copy.60
  (17 shorter events, 0.2 us)
Async XLA Ops:
  6.5 170.8 %copy-start = (bf16[1,8192,160]{1,2,0:T(8,128)(2,1)S(1)}, bf16[1,8192,160]{1,2,0:T(8,128)(2,1)}, u32[]{:S(2)}) copy-start(bf16[1,8192,160]{1,2,0:T(8,128)(2,1)} %param.10) | copy-start | bytes 7864324
  8.4 54.6 %all-to-all-start = ((f32[32,1,256]{2,1,0:T(1,128)}), f32[32,1,256]{2,1,0:T(1,128)S(1)}, u32[]{:S(2)}, u32[]{:S(2)}) async-start(f32[32,1,256]{2,1,0:T(1,128)} %broadcast_in_dim.23), calls=%async_computation | async-start | bytes 65536 | tf_op jit(solution)/shard_map/all_to_all | solution.py:25
  41.6 135.7 %all-gather.2.cloned.1.call-start = ((), (), s32[]{:S(2)}) async-start(), calls=%async_computation.3 | async-start | bytes 4325376 | tf_op jit(solution)/shard_map/all_gather | solution.py:114
  70.3 5.5 %copy-start.3 = (s32[1,256]{1,0:T(1,128)S(1)}, s32[1,256]{1,0:T(1,128)}, u32[]{:S(2)}) copy-start(s32[1,256]{1,0:T(1,128)} %param.15) | copy-start | bytes 3076
  77.3 117.8 %copy-start.4 = (s32[1,8]{1,0:T(1,128)S(1)}, s32[1,8]{1,0:T(1,128)}, u32[]{:S(2)}) copy-start(s32[1,8]{1,0:T(1,128)} %param.14) | copy-start | bytes 100
  183.0 37.6 %all-to-all-start.1 = ((bf16[32,8,160]{2,1,0:T(8,128)(2,1)}), bf16[32,8,160]{2,1,0:T(8,128)(2,1)S(1)}, u32[]{:S(2)}, u32[]{:S(2)}) async-start(bf16[32,8,160]{2,1,0:T(8,128)(2,1)} %bitcast.6), calls=%async_computation.1 | async-start | bytes 262144 | tf_op jit(solution)/shard_map/all_to_all | solution.py:116
  220.7 4.4 copy-start.1
  227.5 187.0 %all-to-all-start.2 = ((bf16[32,8,4096]{2,1,0:T(8,128)(2,1)}), bf16[32,8,4096]{2,1,0:T(8,128)(2,1)}, u32[]{:S(2)}, u32[]{:S(2)}) async-start(bf16[32,8,4096]{2,1,0:T(8,128)(2,1)} %stack.2), calls=%async_computation.2 | async-start | bytes 4194304 | tf_op jit(solution)/shard_map/all_to_all | solution.py:19
  233.0 185.3 %copy-start.2 = (bf16[1,256,256]{2,1,0:T(8,128)(2,1)S(1)}, bf16[1,256,256]{2,1,0:T(8,128)(2,1)}, u32[]{:S(2)}) copy-start(bf16[1,256,256]{2,1,0:T(8,128)(2,1)} %param.8) | copy-start | bytes 393220
  418.4 20.1 %collective-permute-start = (bf16[1,256,256]{2,1,0:T(8,128)(2,1)S(1)}, bf16[1,256,256]{2,1,0:T(8,128)(2,1)S(1)}, u32[]{:S(2)}, u32[]{:S(2)}) collective-permute-start(bf16[1,256,256]{2,1,0:T(8,128)(2,1)S(1)} %fusion.37), channel_id=1, source_target_pairs={{0,32},{32,0},{1,33},{33,1},{2,34},{34,2},{3,35},{35,3},{4,36},{36... | collective-permute-start | bytes 393224 | tf_op jit(solution)/shard_map/ppermute | solution.py:37
Sparse Core Ops, SparseCore 0:
  64.9 112.3 all-gather.1
